TPU v7x, 32 devices: a whole 2x2x4 slice. The times are simulated.
32 devices in a mesh: dp: 16 (over z, y, core), expert: 2 (over x).
Axes of the slice: x: 2, y: 2, z: 4, core: 2. Of those that a mesh axis runs over, the one named last changes fastest.
Arguments:
- tokens: bfloat16 [256, 6144], P('dp', 'expert'), may hold values from -6 to 6
- expert_ids: int32 [256, 2], P('dp'), may hold values from 0 to 7, all different within a row; in each aligned block of 16 rows (0 to 15, 16 to 31, ...) at most 8 rows name the same one
- gate_probs: float32 [256, 2], P('dp'), may hold values from 0.1 to 1
- w_gate: bfloat16 [8, 6144, 8192], P('expert', None, 'dp'), may hold values from -0.078125 to 0.078125
- w_up: bfloat16 [8, 6144, 8192], P('expert', None, 'dp'), may hold values from -0.078125 to 0.078125
- w_down_t: bfloat16 [8, 6144, 8192], P('expert', 'dp'), may hold values from -0.0625 to 0.0625
Outputs:
- mixed: bfloat16 [256, 6144], P('dp', 'expert')
Inputs may be any that keep to these rules, and one draw needn't show every extreme that they name: `expert_ids`: each row names 2 different experts. Among the 16 rows of one index of dp no expert is named more than 8 times, a bound that some block reaches.
All inputs are finite; a program needn't handle non-finite values.
Results may differ from a plain program's by a relative error of at most 0.0057.
Values may be sent and summed in bfloat16 or wider, within the bound.
A program may use at most 128 MiB of HBM per device.

v0:
```python
import jax
import jax.numpy as jnp
from jax import lax
from jax.sharding import PartitionSpec as P


def assignments(expert_ids, experts, capacity):
    flat = expert_ids.reshape(-1)
    onehot = (flat[:, None] == jnp.arange(experts, dtype=jnp.int32)[None, :]).astype(jnp.int32)
    earlier = jnp.cumsum(onehot, axis=0) - onehot
    position = jnp.sum(earlier * onehot, axis=1).reshape(expert_ids.shape)
    expert_hit = (
        expert_ids[:, :, None] == jnp.arange(experts, dtype=jnp.int32)[None, None, :]
    ).astype(jnp.float32)
    slot_hit = (
        position[:, :, None] == jnp.arange(capacity, dtype=jnp.int32)[None, None, :]
    ).astype(jnp.float32)
    return (expert_hit, slot_hit)


def per_device(tokens, expert_ids, gate_probs, w_gate, w_up, w_down_t):
    local_experts = w_gate.shape[0]
    expert_count = lax.axis_size("expert")
    dp_count = lax.axis_size("dp")
    experts = local_experts * expert_count
    capacity = tokens.shape[0] // 2
    expert_hit, slot_hit = assignments(expert_ids, experts, capacity)
    dispatch_map = jnp.einsum("tke,tkc->ect", expert_hit, slot_hit).astype(jnp.bfloat16)
    combine_map = jnp.einsum(
        "tk,tke,tkc->tec", gate_probs, expert_hit, slot_hit, precision=lax.Precision.HIGHEST
    )
    slots = jnp.einsum(
        "ect,td->ecd", dispatch_map, tokens, preferred_element_type=jnp.float32
    ).astype(jnp.bfloat16)
    arrived = lax.all_to_all(slots, "expert", split_axis=0, concat_axis=2, tiled=True)
    piece = lax.all_gather(arrived, "dp", axis=1, tiled=True)
    gate = jnp.einsum("erd,edf->erf", piece, w_gate, preferred_element_type=jnp.float32)
    up = jnp.einsum("erd,edf->erf", piece, w_up, preferred_element_type=jnp.float32)
    hidden = (jax.nn.silu(gate) * up).astype(jnp.bfloat16)
    partial_out = jnp.einsum(
        "erf,edf->erd",
        lax.all_gather(hidden, "dp", axis=2, tiled=True),
        w_down_t,
        preferred_element_type=jnp.float32,
    )
    results = partial_out.astype(jnp.bfloat16).reshape(
        local_experts, dp_count, capacity, w_down_t.shape[1]
    )
    results = lax.all_to_all(results, "dp", split_axis=1, concat_axis=3, tiled=True)
    results = results.reshape(local_experts, capacity, results.shape[3])
    slice_width = tokens.shape[1]
    outgoing = results.reshape(local_experts, capacity, expert_count, slice_width)
    returned = lax.all_to_all(outgoing, "expert", split_axis=2, concat_axis=0, tiled=True)
    returned = returned.reshape(experts, capacity, slice_width)
    mixed = jnp.einsum(
        "tec,ecd->td", combine_map, returned.astype(jnp.float32), precision=lax.Precision.HIGHEST
    )
    return mixed.astype(jnp.bfloat16)


def solution(mesh):
    placed = (
        P("dp", "expert"),
        P("dp", None),
        P("dp", None),
        P("expert", None, "dp"),
        P("expert", None, "dp"),
        P("expert", "dp", None),
    )
    return jax.shard_map(
        per_device, mesh=mesh, in_specs=placed, out_specs=P("dp", "expert"), check_vma=False
    )
```

profile of v0, /device:TPU:0, one launch (start us, length us, event | category | flops | bytes accessed | tf_op | source)
XLA Modules:
  0.0 233.5 jit_solution(2106220213072693453)
XLA Ops:
  6.5 0.0 copy-start
  6.5 0.0 all-gather.3.cloned.1.call-start
  6.5 0.8 copy.17
  7.3 0.1 eq.46
  7.4 0.1 fusion.7
  7.5 0.1 reduce_window_sum.11
  7.5 0.2 select_reduce_fusion
  7.7 0.1 eq.50
  7.8 0.3 fusion.3
  8.1 0.1 copy.20
  8.2 0.0 copy-done
  8.2 0.2 convolution_convert_fusion
  8.5 10.6 %all_to_all.48 = bf16[8,8,3072]{2,1,0:T(8,128)(2,1)S(1)} all-to-all(bf16[8,8,3072]{2,1,0:T(8,128)(2,1)S(1)} %convolution_convert_fusion), channel_id=1, replica_groups=mesh['dp'=16,'expert'=2] {'expert'}, dimensions={0} | all-to-all | bytes 786432 | tf_op jit(solution)/shard_map/all_to_all | solution.py:35
  19.1 0.8 copy.21
  19.9 0.0 all-gather.3.cloned.1.call-update
  19.9 0.0 all-gather.5.cloned.1.call-start
  19.9 62.0 %all-gather.3.cloned.1.call-done = bf16[4,128,6144]{2,1,0:T(8,128)(2,1)} async-done(((bf16[4,8,6144]{2,1,0:T(8,128)(2,1)}), bf16[4,128,6144]{2,1,0:T(8,128)(2,1)}) %all-gather.3.cloned.1.call-update) | async-done | bytes 6291472 | tf_op jit(solution)/shard_map/all_gather | solution.py:36
  81.9 0.0 copy-start.2
  81.9 11.9 %fusion.16 = f32[4,128,512]{2,1,0:T(8,128)S(1)} fusion(bf16[4,128,6144]{2,1,0:T(8,128)(2,1)} %all-gather.3.cloned.1.call-done, bf16[4,6144,512]{2,1,0:T(8,128)(2,1)} %param.9), kind=kOutput, calls=%fused_computation.25 | convolution fusion | flops 3221225472 | bytes 32505856 | tf_op jit(solution)/shard_map/erd,edf->erf/dot_general | solution.py:37
  93.8 0.0 copy-done.2
  93.9 0.0 copy-start.1
  93.9 12.6 %fusion.1 = bf16[4,128,512]{2,1,0:T(8,128)(2,1)} fusion(bf16[4,128,6144]{2,1,0:T(8,128)(2,1)S(1)} %copy-done.2, bf16[4,6144,512]{2,1,0:T(8,128)(2,1)} %param.10, f32[4,128,512]{2,1,0:T(8,128)S(1)} %fusion.16), kind=kOutput, calls=%fused_computation.4 | convolution fusion | flops 3222798336 | bytes 33030144 | tf_op jit(solution)/shard_map/erd,edf->erf/dot_general | solution.py:38
  106.4 0.0 copy-start.3
  106.4 0.0 all-gather.5.cloned.1.call-update
  106.5 76.5 %all-gather.5.cloned.1.call-done = bf16[4,128,8192]{2,1,0:T(8,128)(2,1)} async-done(((bf16[4,128,512]{2,1,0:T(8,128)(2,1)}), bf16[4,128,8192]{2,1,0:T(8,128)(2,1)}) %all-gather.5.cloned.1.call-update) | async-done | bytes 8388624 | tf_op jit(solution)/shard_map/all_gather | solution.py:42
  183.0 14.5 %fusion.2 = bf16[4,16,8,384]{3,2,1,0:T(8,128)(2,1)S(1)} fusion(bf16[4,128,8192]{2,1,0:T(8,128)(2,1)} %all-gather.5.cloned.1.call-done, bf16[4,384,8192]{2,1,0:T(8,128)(2,1)} %param.11), kind=kOutput, calls=%fused_computation.6 | convolution fusion | flops 3221422080 | bytes 33947648 | tf_op jit(solution)/shard_map/erf,edf->erd/dot_general | solution.py:40
  197.5 0.8 copy.22
  198.3 3.6 %all-to-all-start.1 = ((bf16[4,16,8,384]{3,2,0,1:T(8,128)(2,1)}), bf16[4,16,8,384]{3,2,0,1:T(8,128)(2,1)S(1)}, u32[]{:S(2)}, u32[]{:S(2)}) async-start(bf16[4,16,8,384]{3,2,0,1:T(8,128)(2,1)} %copy.22), calls=%async_computation.1 | async-start | bytes 786432 | tf_op jit(solution)/shard_map/all_to_all | solution.py:49
  201.8 0.0 copy-done.3
  201.8 0.1 copy.18
  201.9 12.0 %all-to-all-done.1 = bf16[4,16,8,384]{3,2,0,1:T(8,128)(2,1)S(1)} async-done(((bf16[4,16,8,384]{3,2,0,1:T(8,128)(2,1)}), bf16[4,16,8,384]{3,2,0,1:T(8,128)(2,1)S(1)}, u32[]{:S(2)}, u32[]{:S(2)}) %all-to-all-start.1) | async-done | bytes 393248 | tf_op jit(solution)/shard_map/all_to_all | solution.py:49
  213.9 0.1 copy.23
  214.1 0.1 reshape_reshape.3
  214.2 0.8 copy.24
  215.0 3.5 %all-to-all-start.2 = ((bf16[4,8,2,3072]{3,1,0,2:T(8,128)(2,1)}), bf16[4,8,2,3072]{3,1,0,2:T(8,128)(2,1)S(1)}, u32[]{:S(2)}, u32[]{:S(2)}) async-start(bf16[4,8,2,3072]{3,1,0,2:T(8,128)(2,1)} %copy.24), calls=%async_computation.2 | async-start | bytes 786432 | tf_op jit(solution)/shard_map/all_to_all | solution.py:53
  218.5 0.4 fusion.6
  218.9 0.1 copy.26
  219.0 6.6 %all-to-all-done.2 = bf16[4,8,2,3072]{3,1,0,2:T(8,128)(2,1)S(1)} async-done(((bf16[4,8,2,3072]{3,1,0,2:T(8,128)(2,1)}), bf16[4,8,2,3072]{3,1,0,2:T(8,128)(2,1)S(1)}, u32[]{:S(2)}, u32[]{:S(2)}) %all-to-all-start.2) | async-done | bytes 393248 | tf_op jit(solution)/shard_map/all_to_all | solution.py:53
  225.6 1.1 fusion
  226.7 0.0 copy-done.1
Async XLA Ops:
  6.5 1.7 copy-start
  6.5 75.4 %all-gather.3.cloned.1.call-start = ((), (), s32[]{:S(2)}) async-start(), calls=%async_computation.3 | async-start | bytes 6684672 | tf_op jit(solution)/shard_map/all_gather | solution.py:36
  19.9 163.1 %all-gather.5.cloned.1.call-start = ((), (), s32[]{:S(2)}) async-start(), calls=%async_computation.4 | async-start | bytes 8912896 | tf_op jit(solution)/shard_map/all_gather | solution.py:42
  81.9 11.9 %copy-start.2 = (bf16[4,128,6144]{2,1,0:T(8,128)(2,1)S(1)}, bf16[4,128,6144]{2,1,0:T(8,128)(2,1)}, u32[]{:S(2)}) copy-start(bf16[4,128,6144]{2,1,0:T(8,128)(2,1)} %all-gather.3.cloned.1.call-done) | copy-start | bytes 18874372
  93.9 132.8 %copy-start.1 = (bf16[16,3072]{1,0:T(8,128)(2,1)S(1)}, bf16[16,3072]{1,0:T(8,128)(2,1)}, u32[]{:S(2)}) copy-start(bf16[16,3072]{1,0:T(8,128)(2,1)} %param.6) | copy-start | bytes 294916
  106.4 95.4 %copy-start.3 = (f32[16,2]{0,1:T(2,128)S(1)}, f32[16,2]{0,1:T(2,128)}, u32[]{:S(2)}) copy-start(f32[16,2]{0,1:T(2,128)} %param.8) | copy-start | bytes 388
  198.3 15.7 %all-to-all-start.1 = ((bf16[4,16,8,384]{3,2,0,1:T(8,128)(2,1)}), bf16[4,16,8,384]{3,2,0,1:T(8,128)(2,1)S(1)}, u32[]{:S(2)}, u32[]{:S(2)}) async-start(bf16[4,16,8,384]{3,2,0,1:T(8,128)(2,1)} %copy.22), calls=%async_computation.1 | async-start | bytes 786432 | tf_op jit(solution)/shard_map/all_to_all | solution.py:49
  215.0 10.6 %all-to-all-start.2 = ((bf16[4,8,2,3072]{3,1,0,2:T(8,128)(2,1)}), bf16[4,8,2,3072]{3,1,0,2:T(8,128)(2,1)S(1)}, u32[]{:S(2)}, u32[]{:S(2)}) async-start(bf16[4,8,2,3072]{3,1,0,2:T(8,128)(2,1)} %copy.24), calls=%async_computation.2 | async-start | bytes 786432 | tf_op jit(solution)/shard_map/all_to_all | solution.py:53
Sparse Core Ops, SparseCore 0:
  20.0 61.8 all-gather.2
  106.6 76.3 all-gather.4
where the time goes:
time: 234 us
  waiting for transfers between devices  157 us (67%)
  matrix products  41 us (18%)
  between operations  13.5 us (6%)
  blocking collectives  10.6 us (5%)
  starting transfers between devices  7.06 us (3%)
  local copies, waits for them, and re-layouts  3.83 us (2%)
    all_gather x1, waiting for transfers between devices, per_device(): lax.all_gather(hidden, 'dp', axis=2, tiled=True)  76.5 us
    all_gather x1, waiting for transfers between devices, per_device(): piece = lax.all_gather(arrived, 'dp', axis=1, tiled=True)  62 us
    dot_general x1, matrix products, per_device(): jnp.einsum('erf,edf->erd', lax.all_gather(hidden, 'dp', axis=2, tiled=Tru...  14.5 us
    dot_general x1, matrix products, per_device(): jnp.einsum('erd,edf->erf', piece, w_up, preferred_element_type=jnp.float32)  12.6 us
    all_to_all x1, waiting for transfers between devices, per_device(): lax.all_to_all(results, 'dp', split_axis=1, concat_axis=3, tiled=True)  12 us
    dot_general x1, matrix products, per_device(): jnp.einsum('erd,edf->erf', piece, w_gate, preferred_element_type=jnp.floa...  11.9 us
    all_to_all x1, blocking collectives, per_device(): lax.all_to_all(slots, 'expert', split_axis=0, concat_axis=2, tiled=True)  10.6 us
    all_to_all x1, waiting for transfers between devices, per_device(): lax.all_to_all(outgoing, 'expert', split_axis=2, concat_axis=0, tiled=True)  6.61 us
  transfers between devices with their start and end apart: 4, of which 4 were waited for; matrix products, arithmetic and copies ran while one was open for 0% of the time, Pallas kernels for 0%

commit v1 on v0

--- a/solution.py
+++ b/solution.py
@@ -2,6 +2,27 @@
 import jax.numpy as jnp
 from jax import lax
 from jax.sharding import PartitionSpec as P
+
+
+def note_words(vals, link_axis, message):
+    p_next = lax.axis_size(link_axis)
+    k_now, response, v_now = (p_next, lax.axis_index(link_axis), vals.shape[2])
+    pages = tuple(((q, (q + 1) % k_now) for q in range(k_now)))
+    mixed_arr = k_now // 2
+    sides = tuple(((q, (q - 1) % k_now) for q in range(k_now)))
+    known = wide_out = vals
+    w2 = message(vals, response * v_now)
+    src_i = 1
+    while src_i < mixed_arr + 1:
+        known = lax.ppermute(known, axis_name=link_axis, perm=pages)
+        if src_i < k_now - mixed_arr:
+            wide_out = lax.ppermute(wide_out, axis_name=link_axis, perm=sides)
+            carry_in = message(wide_out, (response + src_i) % k_now * v_now)
+            w2 = w2 + carry_in
+        moved = message(known, (response - src_i) % k_now * v_now)
+        w2 = w2 + moved
+        src_i = src_i + 1
+    return w2
 
 
 def assignments(expert_ids, experts, capacity):
@@ -37,11 +58,15 @@
     gate = jnp.einsum("erd,edf->erf", piece, w_gate, preferred_element_type=jnp.float32)
     up = jnp.einsum("erd,edf->erf", piece, w_up, preferred_element_type=jnp.float32)
     hidden = (jax.nn.silu(gate) * up).astype(jnp.bfloat16)
-    partial_out = jnp.einsum(
-        "erf,edf->erd",
-        lax.all_gather(hidden, "dp", axis=2, tiled=True),
-        w_down_t,
-        preferred_element_type=jnp.float32,
+    partial_out = note_words(
+        hidden,
+        link_axis="dp",
+        message=lambda own_block, offset: jnp.einsum(
+            "erf,edf->erd",
+            own_block,
+            lax.dynamic_slice_in_dim(w_down_t, offset, own_block.shape[2], axis=2),
+            preferred_element_type=jnp.float32,
+        ),
     )
     results = partial_out.astype(jnp.bfloat16).reshape(
         local_experts, dp_count, capacity, w_down_t.shape[1]

time: 234 us -> 253 us (1.081)
  starting transfers between devices: 7.06 us -> 61.6 us
  waiting for transfers between devices: 157 us -> 104 us
  matrix products: 41 us -> 58 us
    all_gather x1 -> x0, waiting for transfers between devices: 76.5 us -> none  [per_device(): lax.all_gather(hidden, 'dp', axis=2, tiled=True)]
    ppermute x0 -> x15, starting transfers between devices: none -> 47.6 us  [the longest x8 29.8 us: note_words(): known = lax.ppermute(known, axis_name=link_axis, perm=pages)]
    ppermute x0 -> x15, waiting for transfers between devices: none -> 23.3 us  [the longest x8 23.2 us: note_words(): known = lax.ppermute(known, axis_name=link_axis, perm=pages)]
    dot_general x1 -> x16, matrix products: 14.5 us -> 32.3 us  [per_device(): jnp.einsum('erf,edf->erd', own_block, lax.dynamic_slice_in_dim(w_down_t,...]
    all_to_all x1, starting transfers between devices: 3.55 us -> 10.6 us  [per_device(): lax.all_to_all(results, 'dp', split_axis=1, concat_axis=3, tiled=True)]
  transfers between devices with their start and end apart: 4 -> 18, of which waited for: 4 -> 11; matrix products, arithmetic and copies ran while one was open for 0% -> 12% of each run, Pallas kernels for 0% -> 0%
where the time goes in v1:
time: 253 us; the launch traced here: 252 us
  waiting for transfers between devices  104 us (41%)
  starting transfers between devices  61.6 us (24%)
  matrix products  58 us (23%)
  between operations  13.6 us (5%)
  blocking collectives  10.6 us (4%)
  local copies, waits for them, and re-layouts  3.88 us (2%)
    all_gather x1, waiting for transfers between devices, per_device(): piece = lax.all_gather(arrived, 'dp', axis=1, tiled=True)  62 us
    dot_general x16, matrix products, per_device(): jnp.einsum('erf,edf->erd', own_block, lax.dynamic_slice_in_dim(w_down_t,...  32.3 us
    ppermute x8, starting transfers between devices, note_words(): known = lax.ppermute(known, axis_name=link_axis, perm=pages)  29.8 us
    ppermute x8, waiting for transfers between devices, note_words(): known = lax.ppermute(known, axis_name=link_axis, perm=pages)  23.2 us
    ppermute x7, starting transfers between devices, note_words(): wide_out = lax.ppermute(wide_out, axis_name=link_axis, perm=sides)  17.7 us
    all_to_all x1, waiting for transfers between devices, per_device(): lax.all_to_all(results, 'dp', split_axis=1, concat_axis=3, tiled=True)  12.1 us
    dot_general x1, matrix products, per_device(): jnp.einsum('erd,edf->erf', piece, w_gate, preferred_element_type=jnp.floa...  11.9 us
    dot_general x1, matrix products, per_device(): jnp.einsum('erd,edf->erf', piece, w_up, preferred_element_type=jnp.float32)  11.7 us
  transfers between devices with their start and end apart: 18, of which 11 were waited for; matrix products, arithmetic and copies ran while one was open for 12% of the time, Pallas kernels for 0%

profile of v1, /device:TPU:0, one launch (start us, length us, event | category | flops | bytes accessed | tf_op | source)
XLA Modules:
  0.0 252.0 jit_solution(17330850615361440236)
XLA Ops:
  6.5 0.8 copy.17
  7.3 0.1 eq.62
  7.4 0.1 fusion.89
  7.5 0.1 reduce_window_sum.11
  7.5 0.2 select_reduce_fusion
  7.7 0.1 eq.66
  7.8 0.3 fusion.85
  8.1 0.1 copy.20
  8.2 0.2 convolution_convert_fusion
  8.5 10.6 %all_to_all.48 = bf16[8,8,3072]{2,1,0:T(8,128)(2,1)S(1)} all-to-all(bf16[8,8,3072]{2,1,0:T(8,128)(2,1)S(1)} %convolution_convert_fusion), channel_id=1, replica_groups=mesh['dp'=16,'expert'=2] {'expert'}, dimensions={0} | all-to-all | bytes 786432 | tf_op jit(solution)/shard_map/all_to_all | solution.py:56
  19.1 0.8 copy.21
  19.9 62.0 %all-gather.2.cloned.1.call-done = bf16[4,128,6144]{2,1,0:T(8,128)(2,1)} async-done(((bf16[4,8,6144]{2,1,0:T(8,128)(2,1)}), bf16[4,128,6144]{2,1,0:T(8,128)(2,1)}) %all-gather.2.cloned.1.call-update) | async-done | bytes 6291472 | tf_op jit(solution)/shard_map/all_gather | solution.py:57
  81.9 11.9 %fusion.114 = f32[4,128,512]{2,1,0:T(8,128)S(1)} fusion(bf16[4,128,6144]{2,1,0:T(8,128)(2,1)} %all-gather.2.cloned.1.call-done, bf16[4,6144,512]{2,1,0:T(8,128)(2,1)} %param.9), kind=kOutput, calls=%fused_computation.88 | convolution fusion | flops 3221225472 | bytes 32505856 | tf_op jit(solution)/shard_map/erd,edf->erf/dot_general | solution.py:58
  93.9 11.7 %fusion.78 = bf16[4,128,512]{2,1,0:T(8,128)(2,1)S(1)} fusion(bf16[4,128,6144]{2,1,0:T(8,128)(2,1)S(1)} %copy-done.2, bf16[4,6144,512]{2,1,0:T(8,128)(2,1)} %param.10, f32[4,128,512]{2,1,0:T(8,128)S(1)} %fusion.114), kind=kOutput, calls=%fused_computation.51 | convolution fusion | flops 3222798336 | bytes 33030144 | tf_op jit(solution)/shard_map/erd,edf->erf/dot_general | solution.py:59
  105.6 0.3 collective-permute-start.1
  105.9 4.2 %collective-permute-start = (bf16[4,128,512]{2,1,0:T(8,128)(2,1)S(1)}, bf16[4,128,512]{2,1,0:T(8,128)(2,1)S(1)}, u32[]{:S(2)}, u32[]{:S(2)}) collective-permute-start(bf16[4,128,512]{2,1,0:T(8,128)(2,1)S(1)} %fusion.78), channel_id=1, source_target_pairs={{0,30},{2,0},{4,2},{6,4},{8,6},{10,8},{12,10},{14,12},{16,14},{18,... | collective-permute-start | bytes 1572872 | tf_op jit(solution)/shard_map/ppermute | solution.py:19
  110.1 2.0 fusion.31
  112.1 5.0 %collective-permute-done.1 = bf16[4,128,512]{2,1,0:T(8,128)(2,1)S(1)} collective-permute-done((bf16[4,128,512]{2,1,0:T(8,128)(2,1)S(1)}, bf16[4,128,512]{2,1,0:T(8,128)(2,1)S(1)}, u32[]{:S(2)}, u32[]{:S(2)}) %collective-permute-start.1) | collective-permute-done | bytes 524320 | tf_op jit(solution)/shard_map/ppermute | solution.py:17
  117.0 1.0 collective-permute-start.3
  118.0 3.4 %collective-permute-start.2 = (bf16[4,128,512]{2,1,0:T(8,128)(2,1)S(1)}, bf16[4,128,512]{2,1,0:T(8,128)(2,1)S(1)}, u32[]{:S(2)}, u32[]{:S(2)}) collective-permute-start(bf16[4,128,512]{2,1,0:T(8,128)(2,1)S(1)} %collective-permute-done), channel_id=1, source_target_pairs={{0,30},{2,0},{4,2},{6,4},{8,6},{10,8},{12,10},{14,12},{16,14},{18,... | collective-permute-start | bytes 1572872 | tf_op jit(solution)/shard_map/ppermute | solution.py:19
  121.5 2.0 fusion.27
  123.5 2.0 fusion.36
  125.5 2.9 %collective-permute-done.3 = bf16[4,128,512]{2,1,0:T(8,128)(2,1)S(1)} collective-permute-done((bf16[4,128,512]{2,1,0:T(8,128)(2,1)S(1)}, bf16[4,128,512]{2,1,0:T(8,128)(2,1)S(1)}, u32[]{:S(2)}, u32[]{:S(2)}) %collective-permute-start.3) | collective-permute-done | bytes 524320 | tf_op jit(solution)/shard_map/ppermute | solution.py:17
  128.4 3.0 %collective-permute-start.5 = (bf16[4,128,512]{2,1,0:T(8,128)(2,1)S(1)}, bf16[4,128,512]{2,1,0:T(8,128)(2,1)S(1)}, u32[]{:S(2)}, u32[]{:S(2)}) collective-permute-start(bf16[4,128,512]{2,1,0:T(8,128)(2,1)S(1)} %collective-permute-done.3), channel_id=1, source_target_pairs={{0,2},{2,4},{4,6},{6,8},{8,10},{10,12},{12,14},{14,16},{16,18},{18... | collective-permute-start | bytes 1572872 | tf_op jit(solution)/shard_map/ppermute | solution.py:17
  131.4 1.4 collective-permute-start.4
  132.9 2.0 fusion.23
  134.9 2.0 fusion.42
  137.0 2.9 %collective-permute-done.5 = bf16[4,128,512]{2,1,0:T(8,128)(2,1)S(1)} collective-permute-done((bf16[4,128,512]{2,1,0:T(8,128)(2,1)S(1)}, bf16[4,128,512]{2,1,0:T(8,128)(2,1)S(1)}, u32[]{:S(2)}, u32[]{:S(2)}) %collective-permute-start.5) | collective-permute-done | bytes 524320 | tf_op jit(solution)/shard_map/ppermute | solution.py:17
  139.8 4.5 %collective-permute-start.7 = (bf16[4,128,512]{2,1,0:T(8,128)(2,1)S(1)}, bf16[4,128,512]{2,1,0:T(8,128)(2,1)S(1)}, u32[]{:S(2)}, u32[]{:S(2)}) collective-permute-start(bf16[4,128,512]{2,1,0:T(8,128)(2,1)S(1)} %collective-permute-done.5), channel_id=1, source_target_pairs={{0,2},{2,4},{4,6},{6,8},{8,10},{10,12},{12,14},{14,16},{16,18},{18... | collective-permute-start | bytes 1572872 | tf_op jit(solution)/shard_map/ppermute | solution.py:17
  144.3 1.6 collective-permute-start.6
  145.9 2.0 fusion.19
  147.9 2.0 fusion.48
  149.9 2.8 %collective-permute-done.7 = bf16[4,128,512]{2,1,0:T(8,128)(2,1)S(1)} collective-permute-done((bf16[4,128,512]{2,1,0:T(8,128)(2,1)S(1)}, bf16[4,128,512]{2,1,0:T(8,128)(2,1)S(1)}, u32[]{:S(2)}, u32[]{:S(2)}) %collective-permute-start.7) | collective-permute-done | bytes 524320 | tf_op jit(solution)/shard_map/ppermute | solution.py:17
  152.8 5.8 %collective-permute-start.9 = (bf16[4,128,512]{2,1,0:T(8,128)(2,1)S(1)}, bf16[4,128,512]{2,1,0:T(8,128)(2,1)S(1)}, u32[]{:S(2)}, u32[]{:S(2)}) collective-permute-start(bf16[4,128,512]{2,1,0:T(8,128)(2,1)S(1)} %collective-permute-done.7), channel_id=1, source_target_pairs={{0,2},{2,4},{4,6},{6,8},{8,10},{10,12},{12,14},{14,16},{16,18},{18... | collective-permute-start | bytes 1572872 | tf_op jit(solution)/shard_map/ppermute | solution.py:17
  158.6 1.5 collective-permute-start.8
  160.1 2.0 fusion.15
  162.1 2.0 fusion.54
  164.1 2.8 %collective-permute-done.9 = bf16[4,128,512]{2,1,0:T(8,128)(2,1)S(1)} collective-permute-done((bf16[4,128,512]{2,1,0:T(8,128)(2,1)S(1)}, bf16[4,128,512]{2,1,0:T(8,128)(2,1)S(1)}, u32[]{:S(2)}, u32[]{:S(2)}) %collective-permute-start.9) | collective-permute-done | bytes 524320 | tf_op jit(solution)/shard_map/ppermute | solution.py:17
  167.0 0.2 collective-permute-start.11
  167.2 5.6 %collective-permute-start.10 = (bf16[4,128,512]{2,1,0:T(8,128)(2,1)S(1)}, bf16[4,128,512]{2,1,0:T(8,128)(2,1)S(1)}, u32[]{:S(2)}, u32[]{:S(2)}) collective-permute-start(bf16[4,128,512]{2,1,0:T(8,128)(2,1)S(1)} %collective-permute-done.8), channel_id=1, source_target_pairs={{0,30},{2,0},{4,2},{6,4},{8,6},{10,8},{12,10},{14,12},{16,14},{18,... | collective-permute-start | bytes 1572872 | tf_op jit(solution)/shard_map/ppermute | solution.py:19
  172.8 2.0 fusion.11
  174.8 2.0 fusion.60
  176.8 2.7 %collective-permute-done.11 = bf16[4,128,512]{2,1,0:T(8,128)(2,1)S(1)} collective-permute-done((bf16[4,128,512]{2,1,0:T(8,128)(2,1)S(1)}, bf16[4,128,512]{2,1,0:T(8,128)(2,1)S(1)}, u32[]{:S(2)}, u32[]{:S(2)}) %collective-permute-start.11) | collective-permute-done | bytes 524320 | tf_op jit(solution)/shard_map/ppermute | solution.py:17
  179.5 7.5 %collective-permute-start.13 = (bf16[4,128,512]{2,1,0:T(8,128)(2,1)S(1)}, bf16[4,128,512]{2,1,0:T(8,128)(2,1)S(1)}, u32[]{:S(2)}, u32[]{:S(2)}) collective-permute-start(bf16[4,128,512]{2,1,0:T(8,128)(2,1)S(1)} %collective-permute-done.11), channel_id=1, source_target_pairs={{0,2},{2,4},{4,6},{6,8},{8,10},{10,12},{12,14},{14,16},{16,18},{18... | collective-permute-start | bytes 1572872 | tf_op jit(solution)/shard_map/ppermute | solution.py:17
  187.0 2.0 fusion.7
  189.0 2.0 fusion.66
  191.1 2.6 %collective-permute-done.13 = bf16[4,128,512]{2,1,0:T(8,128)(2,1)S(1)} collective-permute-done((bf16[4,128,512]{2,1,0:T(8,128)(2,1)S(1)}, bf16[4,128,512]{2,1,0:T(8,128)(2,1)S(1)}, u32[]{:S(2)}, u32[]{:S(2)}) %collective-permute-start.13) | collective-permute-done | bytes 524320 | tf_op jit(solution)/shard_map/ppermute | solution.py:17
  193.7 7.5 %collective-permute-start.14 = (bf16[4,128,512]{2,1,0:T(8,128)(2,1)S(1)}, bf16[4,128,512]{2,1,0:T(8,128)(2,1)S(1)}, u32[]{:S(2)}, u32[]{:S(2)}) collective-permute-start(bf16[4,128,512]{2,1,0:T(8,128)(2,1)S(1)} %collective-permute-done.13), channel_id=1, source_target_pairs={{0,2},{2,4},{4,6},{6,8},{8,10},{10,12},{12,14},{14,16},{16,18},{18... | collective-permute-start | bytes 1572872 | tf_op jit(solution)/shard_map/ppermute | solution.py:17
  201.2 2.0 fusion.3
  203.2 2.0 fusion.72
  205.3 1.5 collective-permute-done.14
  206.8 2.0 fusion.82
  208.9 0.8 copy.22
  209.6 10.6 %all-to-all-start.1 = ((bf16[4,16,8,384]{3,2,0,1:T(8,128)(2,1)}), bf16[4,16,8,384]{3,2,0,1:T(8,128)(2,1)S(1)}, u32[]{:S(2)}, u32[]{:S(2)}) async-start(bf16[4,16,8,384]{3,2,0,1:T(8,128)(2,1)} %copy.22), calls=%async_computation.1 | async-start | bytes 786432 | tf_op jit(solution)/shard_map/all_to_all | solution.py:74
  220.3 0.1 copy.18
  220.4 12.1 %all-to-all-done.1 = bf16[4,16,8,384]{3,2,0,1:T(8,128)(2,1)S(1)} async-done(((bf16[4,16,8,384]{3,2,0,1:T(8,128)(2,1)}), bf16[4,16,8,384]{3,2,0,1:T(8,128)(2,1)S(1)}, u32[]{:S(2)}, u32[]{:S(2)}) %all-to-all-start.1) | async-done | bytes 393248 | tf_op jit(solution)/shard_map/all_to_all | solution.py:74
  232.4 0.1 copy.23
  232.6 0.1 reshape_reshape.3
  232.7 0.8 copy.24
  233.5 3.5 %all-to-all-start.2 = ((bf16[4,8,2,3072]{3,1,0,2:T(8,128)(2,1)}), bf16[4,8,2,3072]{3,1,0,2:T(8,128)(2,1)S(1)}, u32[]{:S(2)}, u32[]{:S(2)}) async-start(bf16[4,8,2,3072]{3,1,0,2:T(8,128)(2,1)} %copy.24), calls=%async_computation.2 | async-start | bytes 786432 | tf_op jit(solution)/shard_map/all_to_all | solution.py:78
  236.9 0.4 fusion.88
  237.4 0.1 copy.26
  237.4 6.6 %all-to-all-done.2 = bf16[4,8,2,3072]{3,1,0,2:T(8,128)(2,1)S(1)} async-done(((bf16[4,8,2,3072]{3,1,0,2:T(8,128)(2,1)}), bf16[4,8,2,3072]{3,1,0,2:T(8,128)(2,1)S(1)}, u32[]{:S(2)}, u32[]{:S(2)}) %all-to-all-start.2) | async-done | bytes 393248 | tf_op jit(solution)/shard_map/all_to_all | solution.py:78
  244.1 1.1 fusion
  (18 shorter events, 0.1 us)
Async XLA Ops:
  6.5 1.7 copy-start
  6.5 75.4 %all-gather.2.cloned.1.call-start = ((), (), s32[]{:S(2)}) async-start(), calls=%async_computation.3 | async-start | bytes 6684672 | tf_op jit(solution)/shard_map/all_gather | solution.py:57
  81.9 11.9 %copy-start.2 = (bf16[4,128,6144]{2,1,0:T(8,128)(2,1)S(1)}, bf16[4,128,6144]{2,1,0:T(8,128)(2,1)}, u32[]{:S(2)}) copy-start(bf16[4,128,6144]{2,1,0:T(8,128)(2,1)} %all-gather.2.cloned.1.call-done) | copy-start | bytes 18874372
  105.6 11.5 %collective-permute-start.1 = (bf16[4,128,512]{2,1,0:T(8,128)(2,1)S(1)}, bf16[4,128,512]{2,1,0:T(8,128)(2,1)S(1)}, u32[]{:S(2)}, u32[]{:S(2)}) collective-permute-start(bf16[4,128,512]{2,1,0:T(8,128)(2,1)S(1)} %fusion.78), channel_id=1, source_target_pairs={{0,2},{2,4},{4,6},{6,8},{8,10},{10,12},{12,14},{14,16},{16,18},{18... | collective-permute-start | bytes 1572872 | tf_op jit(solution)/shard_map/ppermute | solution.py:17
  105.9 12.2 %collective-permute-start = (bf16[4,128,512]{2,1,0:T(8,128)(2,1)S(1)}, bf16[4,128,512]{2,1,0:T(8,128)(2,1)S(1)}, u32[]{:S(2)}, u32[]{:S(2)}) collective-permute-start(bf16[4,128,512]{2,1,0:T(8,128)(2,1)S(1)} %fusion.78), channel_id=1, source_target_pairs={{0,30},{2,0},{4,2},{6,4},{8,6},{10,8},{12,10},{14,12},{16,14},{18,... | collective-permute-start | bytes 1572872 | tf_op jit(solution)/shard_map/ppermute | solution.py:19
  117.0 11.4 %collective-permute-start.3 = (bf16[4,128,512]{2,1,0:T(8,128)(2,1)S(1)}, bf16[4,128,512]{2,1,0:T(8,128)(2,1)S(1)}, u32[]{:S(2)}, u32[]{:S(2)}) collective-permute-start(bf16[4,128,512]{2,1,0:T(8,128)(2,1)S(1)} %collective-permute-done.1), channel_id=1, source_target_pairs={{0,2},{2,4},{4,6},{6,8},{8,10},{10,12},{12,14},{14,16},{16,18},{18... | collective-permute-start | bytes 1572872 | tf_op jit(solution)/shard_map/ppermute | solution.py:17
  118.0 13.4 %collective-permute-start.2 = (bf16[4,128,512]{2,1,0:T(8,128)(2,1)S(1)}, bf16[4,128,512]{2,1,0:T(8,128)(2,1)S(1)}, u32[]{:S(2)}, u32[]{:S(2)}) collective-permute-start(bf16[4,128,512]{2,1,0:T(8,128)(2,1)S(1)} %collective-permute-done), channel_id=1, source_target_pairs={{0,30},{2,0},{4,2},{6,4},{8,6},{10,8},{12,10},{14,12},{16,14},{18,... | collective-permute-start | bytes 1572872 | tf_op jit(solution)/shard_map/ppermute | solution.py:19
  125.5 94.7 %copy-start.3 = (f32[16,2]{0,1:T(2,128)S(1)}, f32[16,2]{0,1:T(2,128)}, u32[]{:S(2)}) copy-start(f32[16,2]{0,1:T(2,128)} %param.8) | copy-start | bytes 388
  128.4 11.4 %collective-permute-start.5 = (bf16[4,128,512]{2,1,0:T(8,128)(2,1)S(1)}, bf16[4,128,512]{2,1,0:T(8,128)(2,1)S(1)}, u32[]{:S(2)}, u32[]{:S(2)}) collective-permute-start(bf16[4,128,512]{2,1,0:T(8,128)(2,1)S(1)} %collective-permute-done.3), channel_id=1, source_target_pairs={{0,2},{2,4},{4,6},{6,8},{8,10},{10,12},{12,14},{14,16},{16,18},{18... | collective-permute-start | bytes 1572872 | tf_op jit(solution)/shard_map/ppermute | solution.py:17
  131.4 12.9 %collective-permute-start.4 = (bf16[4,128,512]{2,1,0:T(8,128)(2,1)S(1)}, bf16[4,128,512]{2,1,0:T(8,128)(2,1)S(1)}, u32[]{:S(2)}, u32[]{:S(2)}) collective-permute-start(bf16[4,128,512]{2,1,0:T(8,128)(2,1)S(1)} %collective-permute-done.2), channel_id=1, source_target_pairs={{0,30},{2,0},{4,2},{6,4},{8,6},{10,8},{12,10},{14,12},{16,14},{18,... | collective-permute-start | bytes 1572872 | tf_op jit(solution)/shard_map/ppermute | solution.py:19
  132.9 112.3 %copy-start.1 = (bf16[16,3072]{1,0:T(8,128)(2,1)S(1)}, bf16[16,3072]{1,0:T(8,128)(2,1)}, u32[]{:S(2)}) copy-start(bf16[16,3072]{1,0:T(8,128)(2,1)} %param.6) | copy-start | bytes 294916
  139.8 12.9 %collective-permute-start.7 = (bf16[4,128,512]{2,1,0:T(8,128)(2,1)S(1)}, bf16[4,128,512]{2,1,0:T(8,128)(2,1)S(1)}, u32[]{:S(2)}, u32[]{:S(2)}) collective-permute-start(bf16[4,128,512]{2,1,0:T(8,128)(2,1)S(1)} %collective-permute-done.5), channel_id=1, source_target_pairs={{0,2},{2,4},{4,6},{6,8},{8,10},{10,12},{12,14},{14,16},{16,18},{18... | collective-permute-start | bytes 1572872 | tf_op jit(solution)/shard_map/ppermute | solution.py:17
  144.3 14.2 %collective-permute-start.6 = (bf16[4,128,512]{2,1,0:T(8,128)(2,1)S(1)}, bf16[4,128,512]{2,1,0:T(8,128)(2,1)S(1)}, u32[]{:S(2)}, u32[]{:S(2)}) collective-permute-start(bf16[4,128,512]{2,1,0:T(8,128)(2,1)S(1)} %collective-permute-done.4), channel_id=1, source_target_pairs={{0,30},{2,0},{4,2},{6,4},{8,6},{10,8},{12,10},{14,12},{16,14},{18,... | collective-permute-start | bytes 1572872 | tf_op jit(solution)/shard_map/ppermute | solution.py:19
  152.8 14.2 %collective-permute-start.9 = (bf16[4,128,512]{2,1,0:T(8,128)(2,1)S(1)}, bf16[4,128,512]{2,1,0:T(8,128)(2,1)S(1)}, u32[]{:S(2)}, u32[]{:S(2)}) collective-permute-start(bf16[4,128,512]{2,1,0:T(8,128)(2,1)S(1)} %collective-permute-done.7), channel_id=1, source_target_pairs={{0,2},{2,4},{4,6},{6,8},{8,10},{10,12},{12,14},{14,16},{16,18},{18... | collective-permute-start | bytes 1572872 | tf_op jit(solution)/shard_map/ppermute | solution.py:17
  158.6 8.6 %collective-permute-start.8 = (bf16[4,128,512]{2,1,0:T(8,128)(2,1)S(1)}, bf16[4,128,512]{2,1,0:T(8,128)(2,1)S(1)}, u32[]{:S(2)}, u32[]{:S(2)}) collective-permute-start(bf16[4,128,512]{2,1,0:T(8,128)(2,1)S(1)} %collective-permute-done.6), channel_id=1, source_target_pairs={{0,30},{2,0},{4,2},{6,4},{8,6},{10,8},{12,10},{14,12},{16,14},{18,... | collective-permute-start | bytes 1572872 | tf_op jit(solution)/shard_map/ppermute | solution.py:19
  167.0 12.5 %collective-permute-start.11 = (bf16[4,128,512]{2,1,0:T(8,128)(2,1)S(1)}, bf16[4,128,512]{2,1,0:T(8,128)(2,1)S(1)}, u32[]{:S(2)}, u32[]{:S(2)}) collective-permute-start(bf16[4,128,512]{2,1,0:T(8,128)(2,1)S(1)} %collective-permute-done.9), channel_id=1, source_target_pairs={{0,2},{2,4},{4,6},{6,8},{8,10},{10,12},{12,14},{14,16},{16,18},{18... | collective-permute-start | bytes 1572872 | tf_op jit(solution)/shard_map/ppermute | solution.py:17
  167.2 19.8 %collective-permute-start.10 = (bf16[4,128,512]{2,1,0:T(8,128)(2,1)S(1)}, bf16[4,128,512]{2,1,0:T(8,128)(2,1)S(1)}, u32[]{:S(2)}, u32[]{:S(2)}) collective-permute-start(bf16[4,128,512]{2,1,0:T(8,128)(2,1)S(1)} %collective-permute-done.8), channel_id=1, source_target_pairs={{0,30},{2,0},{4,2},{6,4},{8,6},{10,8},{12,10},{14,12},{16,14},{18,... | collective-permute-start | bytes 1572872 | tf_op jit(solution)/shard_map/ppermute | solution.py:19
  179.5 14.2 %collective-permute-start.13 = (bf16[4,128,512]{2,1,0:T(8,128)(2,1)S(1)}, bf16[4,128,512]{2,1,0:T(8,128)(2,1)S(1)}, u32[]{:S(2)}, u32[]{:S(2)}) collective-permute-start(bf16[4,128,512]{2,1,0:T(8,128)(2,1)S(1)} %collective-permute-done.11), channel_id=1, source_target_pairs={{0,2},{2,4},{4,6},{6,8},{8,10},{10,12},{12,14},{14,16},{16,18},{18... | collective-permute-start | bytes 1572872 | tf_op jit(solution)/shard_map/ppermute | solution.py:17
  187.0 16.2 %collective-permute-start.12 = (bf16[4,128,512]{2,1,0:T(8,128)(2,1)S(1)}, bf16[4,128,512]{2,1,0:T(8,128)(2,1)S(1)}, u32[]{:S(2)}, u32[]{:S(2)}) collective-permute-start(bf16[4,128,512]{2,1,0:T(8,128)(2,1)S(1)} %collective-permute-done.10), channel_id=1, source_target_pairs={{0,30},{2,0},{4,2},{6,4},{8,6},{10,8},{12,10},{14,12},{16,14},{18,... | collective-permute-start | bytes 1572872 | tf_op jit(solution)/shard_map/ppermute | solution.py:19
  193.7 13.1 %collective-permute-start.14 = (bf16[4,128,512]{2,1,0:T(8,128)(2,1)S(1)}, bf16[4,128,512]{2,1,0:T(8,128)(2,1)S(1)}, u32[]{:S(2)}, u32[]{:S(2)}) collective-permute-start(bf16[4,128,512]{2,1,0:T(8,128)(2,1)S(1)} %collective-permute-done.13), channel_id=1, source_target_pairs={{0,2},{2,4},{4,6},{6,8},{8,10},{10,12},{12,14},{14,16},{16,18},{18... | collective-permute-start | bytes 1572872 | tf_op jit(solution)/shard_map/ppermute | solution.py:17
  209.6 22.8 %all-to-all-start.1 = ((bf16[4,16,8,384]{3,2,0,1:T(8,128)(2,1)}), bf16[4,16,8,384]{3,2,0,1:T(8,128)(2,1)S(1)}, u32[]{:S(2)}, u32[]{:S(2)}) async-start(bf16[4,16,8,384]{3,2,0,1:T(8,128)(2,1)} %copy.22), calls=%async_computation.1 | async-start | bytes 786432 | tf_op jit(solution)/shard_map/all_to_all | solution.py:74
  233.5 10.6 %all-to-all-start.2 = ((bf16[4,8,2,3072]{3,1,0,2:T(8,128)(2,1)}), bf16[4,8,2,3072]{3,1,0,2:T(8,128)(2,1)S(1)}, u32[]{:S(2)}, u32[]{:S(2)}) async-start(bf16[4,8,2,3072]{3,1,0,2:T(8,128)(2,1)} %copy.24), calls=%async_computation.2 | async-start | bytes 786432 | tf_op jit(solution)/shard_map/all_to_all | solution.py:78
Sparse Core Ops, SparseCore 0:
  20.0 61.8 all-gather.1
